TPU v7x, 512 devices: a whole 4x8x8 slice. The times are simulated.
512 devices in a mesh: dp: 64 (over x, z, core), mp: 8 (over y).
Axes of the slice: x: 4, y: 8, z: 8, core: 2. Of those that a mesh axis runs over, the one named last changes fastest.
Arguments:
- ranges: bfloat16 [8192, 2652], P(('dp', 'mp')), may hold values from 0.0099487305 to 1
- board: int32 [8192, 5], P(('dp', 'mp')), may hold values from 0 to 51, as said below
- targets: bfloat16 [8192, 2652], P(('dp', 'mp')), may hold values from -6 to 6
- w_in: bfloat16 [1536, 2704], P(('mp', 'dp')), may hold values from -0.34570312 to 0.34570312
- w_out: bfloat16 [1536, 2652], P(('mp', 'dp')), may hold values from -0.3046875 to 0.3046875
Outputs:
- predicted: bfloat16 [8192, 2652], P(('dp', 'mp'))
- update_in: float32 [1536, 2704], P(('mp', 'dp'))
- update_out: float32 [1536, 2652], P(('mp', 'dp'))
- loss: float32 [], replicated
Inputs may be any that keep to these rules, and one draw needn't show every extreme that they name: `board`: each row holds 5 different cards.
All inputs are finite; a program needn't handle non-finite values.
Results may differ from a plain program's by a relative error of at most 0.014.
Values may be sent and summed in bfloat16 or wider, within the bound.
A program may use at most 64 MiB of HBM per device.

v0:
```python
import jax
import jax.numpy as jnp
from jax import lax
from jax.sharding import Mesh
from jax.sharding import PartitionSpec as P

CARDS = 52
HIDDEN_SIZE = 1536
DP = ("dp_0", "dp_1", "dp_2")
DP_MP = ("dp_0", "dp_1", "dp_2", "mp")
MP_DP = ("mp", "dp_0", "dp_1", "dp_2")


def laid_out(tiles, dim):
    tiles = jnp.moveaxis(tiles, 0, dim)
    dims = tiles.shape
    return tiles.reshape(*dims[:dim], dims[dim] * dims[dim + 1], *dims[dim + 2 :])


def sent_to_all(array, axis):
    peers = lax.axis_size(axis)
    return lax.all_to_all(
        jnp.broadcast_to(array[None], (peers, *array.shape)), axis, 0, 0, tiled=True
    )


def collect(array, axis, dim):
    return laid_out(sent_to_all(array, axis), dim)


def in_blocks(array, dim, peers):
    before, after = (array.shape[:dim], array.shape[dim + 1 :])
    return jnp.moveaxis(array.reshape(*before, peers, -1, *after), dim, 0)


def sent_and_summed(array, axis, dim):
    peers = lax.axis_size(axis)
    tiles = lax.all_to_all(in_blocks(array, dim, peers), axis, 0, 0, tiled=True)
    return jnp.sum(tiles.astype(jnp.float32), axis=0)


def over_axes(array, axes):
    for axis in axes:
        array = lax.psum(array, axis)
    return array


def huber_terms(error_value):
    magnitude = jnp.abs(error_value)
    return jnp.where(magnitude <= 1.0, 0.5 * error_value * error_value, magnitude - 0.5)


def build_features(all_ranges, all_board, card_count):
    card_ids = jnp.arange(card_count, dtype=jnp.int32)
    onehot_board = jnp.sum(
        (all_board[:, :, None] == card_ids[None, None, :]).astype(jnp.float32), axis=1
    ).astype(jnp.bfloat16)
    return jnp.concatenate([all_ranges, onehot_board], axis=1)


def right_product(left_side, right_block):
    return lax.dot_general(
        left_side, right_block, (((1,), (1,)), ((), ())), preferred_element_type=jnp.float32
    )


def left_product(left_side, right_side):
    return lax.dot_general(
        left_side, right_side, (((0,), (0,)), ((), ())), preferred_element_type=jnp.float32
    )


def body(ranges, board, targets, w_in, w_out):
    mp_count = lax.axis_size("mp")
    dp_count = lax.axis_size(DP)
    stored_rows = ranges.shape[0]
    value_width = w_out.shape[1]
    all_ranges, all_board = (collect(ranges, "mp", 0), collect(board, "mp", 0))
    features = build_features(all_ranges, all_board, CARDS)
    local_in = lax.all_gather(w_in, DP, axis=0, tiled=True)
    preact = right_product(features, local_in)
    hidden = jax.nn.gelu(preact).astype(jnp.bfloat16)
    local_out = lax.all_gather(w_out, DP, axis=0, tiled=True)
    partial_value = jnp.dot(hidden, local_out, preferred_element_type=jnp.float32)
    stacked = partial_value.astype(jnp.bfloat16).reshape(mp_count, stored_rows, value_width)
    received = lax.all_to_all(stacked, "mp", split_axis=0, concat_axis=0, tiled=True)
    summed = jnp.sum(received.astype(jnp.float32), axis=0)
    error_value = summed - targets.astype(jnp.float32)
    own_grad = jnp.clip(error_value, -1.0, 1.0).astype(jnp.bfloat16)
    out_grad = collect(own_grad, "mp", 0)
    predicted = summed.astype(jnp.bfloat16)
    loss_part = jnp.sum(huber_terms(error_value))
    grad_out = sent_and_summed(left_product(hidden, out_grad).astype(jnp.bfloat16), DP, 0)
    hidden_grad = right_product(out_grad, local_out)
    unused_value, gelu_back = jax.vjp(jax.nn.gelu, preact)
    preact_grad = gelu_back(hidden_grad)[0].astype(jnp.bfloat16)
    grad_in = sent_and_summed(left_product(preact_grad, features).astype(jnp.bfloat16), DP, 0)
    square_part = jnp.sum(grad_in * grad_in) + jnp.sum(grad_out * grad_out)
    loss_total, square_total = (over_axes(loss_part, DP_MP), over_axes(square_part, DP_MP))
    count_params = HIDDEN_SIZE * (w_in.shape[1] + value_width)
    scale = lax.rsqrt(square_total / count_params + 1e-06)
    loss = loss_total / (stored_rows * mp_count * dp_count * value_width)
    return (predicted, grad_in * scale, grad_out * scale, loss)


def solution(mesh):
    split = Mesh(mesh.devices.reshape(4, 8, 2, mesh.shape["mp"]), ("dp_0", "dp_1", "dp_2", "mp"))
    placed = (P(DP_MP, None), P(DP_MP, None), P(DP_MP, None), P(MP_DP, None), P(MP_DP, None))
    return jax.shard_map(
        body,
        mesh=split,
        in_specs=placed,
        out_specs=(P(DP_MP, None), P(MP_DP, None), P(MP_DP, None), P()),
        check_vma=False,
    )
```

profile of v0, /device:TPU:8, one launch (start us, length us, event | category | flops | bytes accessed | tf_op | source)
XLA Modules:
  0.0 324.2 jit_solution(1523296444616732126)
XLA Ops:
  0.6 0.7 broadcast_in_dim.7
  1.3 14.7 %all_to_all.30 = s32[8,16,5]{1,2,0:T(8,128)S(1)} all-to-all(s32[8,16,5]{1,2,0:T(8,128)S(1)} %broadcast_in_dim.7), channel_id=1, replica_groups=mesh['dp_0'=4,'dp_1'=8,'dp_2'=2,'mp'=8] {'mp'}, dimensions={0} | all-to-all | bytes 5120 | tf_op jit(solution)/shard_map/all_to_all | solution.py:22
  16.1 1.8 broadcast_in_dim.6
  17.9 4.9 %all-to-all-start = ((bf16[8,16,2652]{2,1,0:T(8,128)(2,1)}), bf16[8,16,2652]{2,1,0:T(8,128)(2,1)S(1)}, u32[]{:S(2)}, u32[]{:S(2)}) async-start(bf16[8,16,2652]{2,1,0:T(8,128)(2,1)} %broadcast_in_dim.6), calls=%async_computation | async-start | bytes 1376256 | tf_op jit(solution)/shard_map/all_to_all | solution.py:22
  22.8 55.9 %all-gather = bf16[64,3,2704]{2,1,0:T(4,128)(2,1)S(1)} all-gather(bf16[1,3,2704]{2,1,0:T(4,128)(2,1)S(1)} %bitcast.17), channel_id=1, replica_groups=mesh['dp_0'=4,'dp_1'=8,'dp_2'=2,'mp'=8] {'dp_0','dp_1','dp_2'}, dimensions={0}, use_global_device_ids=true | all-gather | bytes 1054560 | tf_op jit(solution)/shard_map/all_gather | solution.py:80
  78.7 1.7 reshape.33
  80.4 49.7 %all-gather.1 = bf16[64,3,2652]{2,1,0:T(4,128)(2,1)S(1)} all-gather(bf16[1,3,2652]{2,1,0:T(4,128)(2,1)S(1)} %bitcast.18), channel_id=1, replica_groups=mesh['dp_0'=4,'dp_1'=8,'dp_2'=2,'mp'=8] {'dp_0','dp_1','dp_2'}, dimensions={0}, use_global_device_ids=true | all-gather | bytes 1034280 | tf_op jit(solution)/shard_map/all_gather | solution.py:83
  130.1 0.9 reshape.35
  131.3 1.9 fusion
  133.2 0.7 convolution_convert_fusion.2
  134.2 27.2 %all_to_all.31 = bf16[8,16,2652]{2,1,0:T(8,128)(2,1)S(1)} all-to-all(bf16[8,16,2652]{2,1,0:T(8,128)(2,1)S(1)} %bitcast.16), channel_id=1, replica_groups=mesh['dp_0'=4,'dp_1'=8,'dp_2'=2,'mp'=8] {'mp'}, dimensions={0} | all-to-all | bytes 1357824 | tf_op jit(solution)/shard_map/all_to_all | solution.py:86
  161.6 1.3 fusion.2
  162.9 23.8 %all_to_all.32 = bf16[8,16,2652]{2,1,0:T(8,128)(2,1)S(1)} all-to-all(bf16[8,16,2652]{2,1,0:T(8,128)(2,1)S(1)} %broadcast_in_dim.8), channel_id=1, replica_groups=mesh['dp_0'=4,'dp_1'=8,'dp_2'=2,'mp'=8] {'mp'}, dimensions={0} | all-to-all | bytes 1357824 | tf_op jit(solution)/shard_map/all_to_all | solution.py:22
  187.1 1.3 reshape.31
  188.4 5.3 %all-to-all-start.5 = ((bf16[64,3,2652]{2,1,0:T(4,128)(2,1)}), bf16[64,3,2652]{2,1,0:T(4,128)(2,1)S(1)}, u32[]{:S(2)}, u32[]{:S(2)}) async-start(bf16[64,3,2652]{2,1,0:T(4,128)(2,1)} %reshape.31), calls=%async_computation.5 | async-start | bytes 2752512 | tf_op jit(solution)/shard_map/all_to_all | solution.py:38
  193.7 3.4 %convolution_convert_fusion.1 = bf16[192,2704]{1,0:T(8,128)(2,1)} fusion(bf16[128,52]{1,0:T(8,128)(2,1)S(1)} %copy.17, bf16[128,2652]{1,0:T(8,128)(2,1)} %bitcast.15, f32[128,192]{0,1:T(8,128)S(1)} %fusion, bf16[128,2652]{1,0:T(8,128)(2,1)S(1)} %bitcast.13, bf16[192,2652]{1,0:T(8,128)(2,1)S(1)} %reshape.35), kind=kOutput, calls=%fused_computation.1 | convolution fusion | flops 265653248 | bytes 3526144 | tf_op jit(solution)/shard_map/dot_general | solution.py:68
  197.1 3.6 %reshape.30 = bf16[64,3,2704]{2,1,0:T(4,128)(2,1)} reshape(bf16[192,2704]{1,0:T(8,128)(2,1)} %convolution_convert_fusion.1) | data formatting | bytes 2076672 | tf_op jit(solution)/shard_map/reshape | solution.py:33
  200.7 27.9 %all-to-all-done.5 = bf16[64,3,2652]{2,1,0:T(4,128)(2,1)S(1)} async-done(((bf16[64,3,2652]{2,1,0:T(4,128)(2,1)}), bf16[64,3,2652]{2,1,0:T(4,128)(2,1)S(1)}, u32[]{:S(2)}, u32[]{:S(2)}) %all-to-all-start.5) | async-done | bytes 1018400 | tf_op jit(solution)/shard_map/all_to_all | solution.py:38
  228.6 6.8 %all-to-all-start.4 = ((bf16[64,3,2704]{2,1,0:T(4,128)(2,1)}), bf16[64,3,2704]{2,1,0:T(4,128)(2,1)S(1)}, u32[]{:S(2)}, u32[]{:S(2)}) async-start(bf16[64,3,2704]{2,1,0:T(4,128)(2,1)} %reshape.30), calls=%async_computation.4 | async-start | bytes 2883584 | tf_op jit(solution)/shard_map/all_to_all | solution.py:38
  236.6 35.1 %all-to-all-done.4 = bf16[64,3,2704]{2,1,0:T(4,128)(2,1)S(1)} async-done(((bf16[64,3,2704]{2,1,0:T(4,128)(2,1)}), bf16[64,3,2704]{2,1,0:T(4,128)(2,1)S(1)}, u32[]{:S(2)}, u32[]{:S(2)}) %all-to-all-start.4) | async-done | bytes 1038368 | tf_op jit(solution)/shard_map/all_to_all | solution.py:38
  274.2 10.1 %all-reduce.2 = (f32[]{:T(128)}, f32[]{:T(128)}) all-reduce(f32[]{:T(128)S(6)} %add.34, f32[]{:T(128)} %get-tuple-element.12), channel_id=1, replica_groups=mesh['dp_0'=4,'dp_1'=8,'dp_2'=2,'mp'=8] {'dp_0'}, use_global_device_ids=true, to_apply=%region_6.7 | all-reduce | flops 2 | bytes 16 | tf_op jit(solution)/shard_map/psum | solution.py:44
  284.3 16.9 %all-reduce.1 = (f32[]{:T(128)}, f32[]{:T(128)}) all-reduce(f32[]{:T(128)} %get-tuple-element.8, f32[]{:T(128)} %get-tuple-element.9), channel_id=1, replica_groups=mesh['dp_0'=4,'dp_1'=8,'dp_2'=2,'mp'=8] {'dp_1'}, use_global_device_ids=true, to_apply=%region_7.8 | all-reduce | flops 2 | bytes 16 | tf_op jit(solution)/shard_map/psum | solution.py:44
  301.2 3.1 all-reduce.3
  304.2 16.2 %all-reduce = (f32[]{:T(128)}, f32[]{:T(128)}) all-reduce(f32[]{:T(128)} %get-tuple-element.10, f32[]{:T(128)} %get-tuple-element.11), channel_id=1, replica_groups=mesh['dp_0'=4,'dp_1'=8,'dp_2'=2,'mp'=8] {'mp'}, use_global_device_ids=true, to_apply=%region_9.10 | all-reduce | flops 2 | bytes 16 | tf_op jit(solution)/shard_map/psum | solution.py:44
  (23 shorter events, 4.8 us)
Async XLA Ops:
  0.6 22.1 %copy-start.2 = (bf16[3,2704]{1,0:T(4,128)(2,1)S(1)}, bf16[3,2704]{1,0:T(4,128)(2,1)}, u32[]{:S(2)}) copy-start(bf16[3,2704]{1,0:T(4,128)(2,1)} %param.8) | copy-start | bytes 48676
  17.9 113.4 %all-to-all-start = ((bf16[8,16,2652]{2,1,0:T(8,128)(2,1)}), bf16[8,16,2652]{2,1,0:T(8,128)(2,1)S(1)}, u32[]{:S(2)}, u32[]{:S(2)}) async-start(bf16[8,16,2652]{2,1,0:T(8,128)(2,1)} %broadcast_in_dim.6), calls=%async_computation | async-start | bytes 1376256 | tf_op jit(solution)/shard_map/all_to_all | solution.py:22
  78.6 1.7 copy-start.3
  131.3 31.7 %copy-start = (bf16[8,16,2652]{2,1,0:T(8,128)(2,1)}, bf16[8,16,2652]{2,1,0:T(8,128)(2,1)S(1)}, u32[]{:S(2)}) copy-start(bf16[8,16,2652]{2,1,0:T(8,128)(2,1)S(1)} %all-to-all-done) | copy-start | bytes 2036740
  134.2 27.3 %copy-start.1 = (bf16[16,2652]{1,0:T(8,128)(2,1)S(1)}, bf16[16,2652]{1,0:T(8,128)(2,1)}, u32[]{:S(2)}) copy-start(bf16[16,2652]{1,0:T(8,128)(2,1)} %param.7) | copy-start | bytes 254596
  188.4 40.1 %all-to-all-start.5 = ((bf16[64,3,2652]{2,1,0:T(4,128)(2,1)}), bf16[64,3,2652]{2,1,0:T(4,128)(2,1)S(1)}, u32[]{:S(2)}, u32[]{:S(2)}) async-start(bf16[64,3,2652]{2,1,0:T(4,128)(2,1)} %reshape.31), calls=%async_computation.5 | async-start | bytes 2752512 | tf_op jit(solution)/shard_map/all_to_all | solution.py:38
  228.6 43.1 %all-to-all-start.4 = ((bf16[64,3,2704]{2,1,0:T(4,128)(2,1)}), bf16[64,3,2704]{2,1,0:T(4,128)(2,1)S(1)}, u32[]{:S(2)}, u32[]{:S(2)}) async-start(bf16[64,3,2704]{2,1,0:T(4,128)(2,1)} %reshape.30), calls=%async_computation.4 | async-start | bytes 2883584 | tf_op jit(solution)/shard_map/all_to_all | solution.py:38
where the time goes:
time: 325 us; the launch traced here: 324 us
  blocking collectives  218 us (67%)
  waiting for transfers between devices  62.9 us (19%)
  starting transfers between devices  17 us (5%)
  local copies, waits for them, and re-layouts  10.7 us (3%)
  matrix products  6.4 us (2%)
  other arithmetic  5.09 us (2%)
  between operations  4.52 us (1%)
    all_to_all x2, waiting for transfers between devices, sent_and_summed(): tiles = lax.all_to_all(in_blocks(array, dim, peers), axis, 0, 0, tiled=True)  62.9 us
    all_gather x1, blocking collectives, body(): local_in = lax.all_gather(w_in, DP, axis=0, tiled=True)  55.9 us
    all_gather x1, blocking collectives, body(): local_out = lax.all_gather(w_out, DP, axis=0, tiled=True)  49.7 us
    psum x4, blocking collectives, over_axes(): array = lax.psum(array, axis)  46.3 us
    all_to_all x2, blocking collectives, sent_to_all(): lax.all_to_all(jnp.broadcast_to(array[None], (peers, *array.shape)), axis...  38.5 us
    all_to_all x1, blocking collectives, body(): lax.all_to_all(stacked, 'mp', split_axis=0, concat_axis=0, tiled=True)  27.2 us
    all_to_all x2, starting transfers between devices, sent_and_summed(): tiles = lax.all_to_all(in_blocks(array, dim, peers), axis, 0, 0, tiled=True)  12.1 us
  transfers between devices with their start and end apart: 3, of which 2 were waited for; matrix products, arithmetic and copies ran while one was open for 3% of the time, Pallas kernels for 0%

commit v1 on v0

--- a/solution.py
+++ b/solution.py
@@ -77,7 +77,10 @@
     value_width = w_out.shape[1]
     all_ranges, all_board = (collect(ranges, "mp", 0), collect(board, "mp", 0))
     features = build_features(all_ranges, all_board, CARDS)
-    local_in = lax.all_gather(w_in, DP, axis=0, tiled=True)
+    b_next = lax.psum(1, DP)
+    odd = jnp.stack(b_next * [w_in])
+    s_next = lax.all_to_all(odd, axis_name=DP, split_axis=0, concat_axis=0)
+    local_in = jnp.concatenate(s_next, 0)
     preact = right_product(features, local_in)
     hidden = jax.nn.gelu(preact).astype(jnp.bfloat16)
     local_out = lax.all_gather(w_out, DP, axis=0, tiled=True)

time: 325 us -> 327 us (level)
    all_gather x1 -> x0, blocking collectives: 55.9 us -> none  [body(): local_in = lax.all_gather(w_in, DP, axis=0, tiled=True)]
    all_to_all x0 -> x1, blocking collectives: none -> 49.2 us  [body(): s_next = lax.all_to_all(odd, axis_name=DP, split_axis=0, concat_axis=0)]
    all_gather x1, blocking collectives: 49.7 us -> 54 us  [body(): local_out = lax.all_gather(w_out, DP, axis=0, tiled=True)]
  transfers between devices with their start and end apart: 3 -> 3, of which waited for: 2 -> 2; matrix products, arithmetic and copies ran while one was open for 3% -> 4% of each run, Pallas kernels for 0% -> 0%
where the time goes in v1:
time: 327 us; the launch traced here: 326 us
  blocking collectives  215 us (66%)
  waiting for transfers between devices  62.9 us (19%)
  starting transfers between devices  18.9 us (6%)
  local copies, waits for them, and re-layouts  12.6 us (4%)
  matrix products  6.4 us (2%)
  other arithmetic  5.09 us (2%)
  between operations  4.51 us (1%)
    all_to_all x2, waiting for transfers between devices, sent_and_summed(): tiles = lax.all_to_all(in_blocks(array, dim, peers), axis, 0, 0, tiled=True)  62.9 us
    all_gather x1, blocking collectives, body(): local_out = lax.all_gather(w_out, DP, axis=0, tiled=True)  54 us
    all_to_all x1, blocking collectives, body(): s_next = lax.all_to_all(odd, axis_name=DP, split_axis=0, concat_axis=0)  49.2 us
    psum x4, blocking collectives, over_axes(): array = lax.psum(array, axis)  46.3 us
    all_to_all x2, blocking collectives, sent_to_all(): lax.all_to_all(jnp.broadcast_to(array[None], (peers, *array.shape)), axis...  38.5 us
    all_to_all x1, blocking collectives, body(): lax.all_to_all(stacked, 'mp', split_axis=0, concat_axis=0, tiled=True)  27.2 us
    all_to_all x2, starting transfers between devices, sent_and_summed(): tiles = lax.all_to_all(in_blocks(array, dim, peers), axis, 0, 0, tiled=True)  14 us
  transfers between devices with their start and end apart: 3, of which 2 were waited for; matrix products, arithmetic and copies ran while one was open for 4% of the time, Pallas kernels for 0%

profile of v1, /device:TPU:8, one launch (start us, length us, event | category | flops | bytes accessed | tf_op | source)
XLA Modules:
  0.0 325.6 jit_solution(6803625176636629023)
XLA Ops:
  0.6 0.7 broadcast_in_dim.7
  1.3 14.7 %all_to_all.35 = s32[8,16,5]{1,2,0:T(8,128)S(1)} all-to-all(s32[8,16,5]{1,2,0:T(8,128)S(1)} %broadcast_in_dim.7), channel_id=1, replica_groups=mesh['dp_0'=4,'dp_1'=8,'dp_2'=2,'mp'=8] {'mp'}, dimensions={0} | all-to-all | bytes 5120 | tf_op jit(solution)/shard_map/all_to_all | solution.py:22
  16.0 1.1 stack.2
  17.2 49.2 %all_to_all.36 = bf16[64,3,2704]{2,1,0:T(4,128)(2,1)S(1)} all-to-all(bf16[64,3,2704]{2,1,0:T(4,128)(2,1)S(1)} %stack.2), channel_id=1, replica_groups=mesh['dp_0'=4,'dp_1'=8,'dp_2'=2,'mp'=8] {'dp_0','dp_1','dp_2'}, dimensions={0} | all-to-all | bytes 2076672 | tf_op jit(solution)/shard_map/all_to_all | solution.py:82
  66.3 0.9 broadcast_in_dim.6
  67.2 4.9 %all-to-all-start = ((bf16[8,16,2652]{2,1,0:T(8,128)(2,1)}), bf16[8,16,2652]{2,1,0:T(8,128)(2,1)S(1)}, u32[]{:S(2)}, u32[]{:S(2)}) async-start(bf16[8,16,2652]{2,1,0:T(8,128)(2,1)} %broadcast_in_dim.6), calls=%async_computation | async-start | bytes 1376256 | tf_op jit(solution)/shard_map/all_to_all | solution.py:22
  72.1 54.0 %all-gather = bf16[64,3,2652]{2,1,0:T(4,128)(2,1)} all-gather(bf16[1,3,2652]{2,1,0:T(4,128)(2,1)S(1)} %bitcast.16), channel_id=1, replica_groups=mesh['dp_0'=4,'dp_1'=8,'dp_2'=2,'mp'=8] {'dp_0','dp_1','dp_2'}, dimensions={0}, use_global_device_ids=true | all-gather | bytes 1034280 | tf_op jit(solution)/shard_map/all_gather | solution.py:86
  126.2 2.6 reshape.39
  129.0 1.7 reshape.33
  130.8 1.9 fusion
  133.7 27.2 %all_to_all.37 = bf16[8,16,2652]{2,1,0:T(8,128)(2,1)S(1)} all-to-all(bf16[8,16,2652]{2,1,0:T(8,128)(2,1)S(1)} %bitcast.15), channel_id=1, replica_groups=mesh['dp_0'=4,'dp_1'=8,'dp_2'=2,'mp'=8] {'mp'}, dimensions={0} | all-to-all | bytes 1357824 | tf_op jit(solution)/shard_map/all_to_all | solution.py:89
  161.1 1.3 fusion.2
  162.4 23.8 %all_to_all.38 = bf16[8,16,2652]{2,1,0:T(8,128)(2,1)S(1)} all-to-all(bf16[8,16,2652]{2,1,0:T(8,128)(2,1)S(1)} %broadcast_in_dim.8), channel_id=1, replica_groups=mesh['dp_0'=4,'dp_1'=8,'dp_2'=2,'mp'=8] {'mp'}, dimensions={0} | all-to-all | bytes 1357824 | tf_op jit(solution)/shard_map/all_to_all | solution.py:22
  186.6 1.3 reshape.37
  187.9 7.2 %all-to-all-start.6 = ((bf16[64,3,2652]{2,1,0:T(4,128)(2,1)}), bf16[64,3,2652]{2,1,0:T(4,128)(2,1)S(1)}, u32[]{:S(2)}, u32[]{:S(2)}) async-start(bf16[64,3,2652]{2,1,0:T(4,128)(2,1)} %reshape.37), calls=%async_computation.6 | async-start | bytes 2752512 | tf_op jit(solution)/shard_map/all_to_all | solution.py:38
  195.1 3.4 %convolution_convert_fusion.1 = bf16[192,2704]{1,0:T(8,128)(2,1)} fusion(bf16[128,52]{1,0:T(8,128)(2,1)S(1)} %copy.17, bf16[128,2652]{1,0:T(8,128)(2,1)} %bitcast.14, f32[128,192]{0,1:T(8,128)S(1)} %fusion, bf16[128,2652]{1,0:T(8,128)(2,1)S(1)} %bitcast.12, bf16[192,2652]{1,0:T(8,128)(2,1)S(1)} %reshape.39), kind=kOutput, calls=%fused_computation.1 | convolution fusion | flops 265653248 | bytes 3526144 | tf_op jit(solution)/shard_map/dot_general | solution.py:68
  198.5 3.6 %reshape.36 = bf16[64,3,2704]{2,1,0:T(4,128)(2,1)} reshape(bf16[192,2704]{1,0:T(8,128)(2,1)} %convolution_convert_fusion.1) | data formatting | bytes 2076672 | tf_op jit(solution)/shard_map/reshape | solution.py:33
  202.1 27.9 %all-to-all-done.6 = bf16[64,3,2652]{2,1,0:T(4,128)(2,1)S(1)} async-done(((bf16[64,3,2652]{2,1,0:T(4,128)(2,1)}), bf16[64,3,2652]{2,1,0:T(4,128)(2,1)S(1)}, u32[]{:S(2)}, u32[]{:S(2)}) %all-to-all-start.6) | async-done | bytes 1018400 | tf_op jit(solution)/shard_map/all_to_all | solution.py:38
  230.0 6.8 %all-to-all-start.5 = ((bf16[64,3,2704]{2,1,0:T(4,128)(2,1)}), bf16[64,3,2704]{2,1,0:T(4,128)(2,1)S(1)}, u32[]{:S(2)}, u32[]{:S(2)}) async-start(bf16[64,3,2704]{2,1,0:T(4,128)(2,1)} %reshape.36), calls=%async_computation.5 | async-start | bytes 2883584 | tf_op jit(solution)/shard_map/all_to_all | solution.py:38
  238.0 35.1 %all-to-all-done.5 = bf16[64,3,2704]{2,1,0:T(4,128)(2,1)S(1)} async-done(((bf16[64,3,2704]{2,1,0:T(4,128)(2,1)}), bf16[64,3,2704]{2,1,0:T(4,128)(2,1)S(1)}, u32[]{:S(2)}, u32[]{:S(2)}) %all-to-all-start.5) | async-done | bytes 1038368 | tf_op jit(solution)/shard_map/all_to_all | solution.py:38
  275.6 10.1 %all-reduce.2 = (f32[]{:T(128)}, f32[]{:T(128)}) all-reduce(f32[]{:T(128)S(6)} %add.34, f32[]{:T(128)} %get-tuple-element.12), channel_id=1, replica_groups=mesh['dp_0'=4,'dp_1'=8,'dp_2'=2,'mp'=8] {'dp_0'}, use_global_device_ids=true, to_apply=%region_6.7 | all-reduce | flops 2 | bytes 16 | tf_op jit(solution)/shard_map/psum | solution.py:44
  285.7 16.9 %all-reduce.1 = (f32[]{:T(128)}, f32[]{:T(128)}) all-reduce(f32[]{:T(128)} %get-tuple-element.8, f32[]{:T(128)} %get-tuple-element.9), channel_id=1, replica_groups=mesh['dp_0'=4,'dp_1'=8,'dp_2'=2,'mp'=8] {'dp_1'}, use_global_device_ids=true, to_apply=%region_7.8 | all-reduce | flops 2 | bytes 16 | tf_op jit(solution)/shard_map/psum | solution.py:44
  302.6 3.1 all-reduce.3
  305.7 16.2 %all-reduce = (f32[]{:T(128)}, f32[]{:T(128)}) all-reduce(f32[]{:T(128)} %get-tuple-element.10, f32[]{:T(128)} %get-tuple-element.11), channel_id=1, replica_groups=mesh['dp_0'=4,'dp_1'=8,'dp_2'=2,'mp'=8] {'mp'}, use_global_device_ids=true, to_apply=%region_9.10 | all-reduce | flops 2 | bytes 16 | tf_op jit(solution)/shard_map/psum | solution.py:44
  (24 shorter events, 5.5 us)
Async XLA Ops:
  17.1 49.2 %copy-start.1 = (bf16[16,2652]{1,0:T(8,128)(2,1)S(1)}, bf16[16,2652]{1,0:T(8,128)(2,1)}, u32[]{:S(2)}) copy-start(bf16[16,2652]{1,0:T(8,128)(2,1)} %param.5) | copy-start | bytes 254596
  66.3 5.8 %copy-start.3 = (bf16[3,2652]{1,0:T(4,128)(2,1)S(1)}, bf16[3,2652]{1,0:T(4,128)(2,1)}, u32[]{:S(2)}) copy-start(bf16[3,2652]{1,0:T(4,128)(2,1)} %param.9) | copy-start | bytes 47740
  67.2 63.5 %all-to-all-start = ((bf16[8,16,2652]{2,1,0:T(8,128)(2,1)}), bf16[8,16,2652]{2,1,0:T(8,128)(2,1)S(1)}, u32[]{:S(2)}, u32[]{:S(2)}) async-start(bf16[8,16,2652]{2,1,0:T(8,128)(2,1)} %broadcast_in_dim.6), calls=%async_computation | async-start | bytes 1376256 | tf_op jit(solution)/shard_map/all_to_all | solution.py:22
  130.8 31.6 %copy-start = (bf16[8,16,2652]{2,1,0:T(8,128)(2,1)}, bf16[8,16,2652]{2,1,0:T(8,128)(2,1)S(1)}, u32[]{:S(2)}) copy-start(bf16[8,16,2652]{2,1,0:T(8,128)(2,1)S(1)} %all-to-all-done) | copy-start | bytes 2036740
  133.7 27.3 %copy-start.2 = (bf16[16,2652]{1,0:T(8,128)(2,1)S(1)}, bf16[16,2652]{1,0:T(8,128)(2,1)}, u32[]{:S(2)}) copy-start(bf16[16,2652]{1,0:T(8,128)(2,1)} %param.7) | copy-start | bytes 254596
  187.9 42.1 %all-to-all-start.6 = ((bf16[64,3,2652]{2,1,0:T(4,128)(2,1)}), bf16[64,3,2652]{2,1,0:T(4,128)(2,1)S(1)}, u32[]{:S(2)}, u32[]{:S(2)}) async-start(bf16[64,3,2652]{2,1,0:T(4,128)(2,1)} %reshape.37), calls=%async_computation.6 | async-start | bytes 2752512 | tf_op jit(solution)/shard_map/all_to_all | solution.py:38
  230.0 43.1 %all-to-all-start.5 = ((bf16[64,3,2704]{2,1,0:T(4,128)(2,1)}), bf16[64,3,2704]{2,1,0:T(4,128)(2,1)S(1)}, u32[]{:S(2)}, u32[]{:S(2)}) async-start(bf16[64,3,2704]{2,1,0:T(4,128)(2,1)} %reshape.36), calls=%async_computation.5 | async-start | bytes 2883584 | tf_op jit(solution)/shard_map/all_to_all | solution.py:38
